TPU v7x, 32 devices: a whole 2x2x4 slice. The times are simulated.
32 devices in a mesh: tm: 8 (over z, y), space: 4 (over x, core).
Axes of the slice: x: 2, y: 2, z: 4, core: 2. Of those that a mesh axis runs over, the one named last changes fastest.
Arguments:
- observed: float32 [64, 512, 128], P('tm', 'space'), may hold values from -6 to 6
- gain: float32 [4, 128, 128], P('space'), may hold values from -0.15625 to 0.15625
- trans: float32 [4, 384, 128], P('space'), may hold values from -1 to 1
- dynamics: float32 [4, 384, 128], P('space'), may hold values from -1 to 1
- smooth_gain: float32 [4, 384, 128], P('space'), may hold values from -1 to 1
Outputs:
- filtered: float32 [64, 512, 128], P('tm', 'space')
- smoothed: float32 [64, 512, 128], P('tm', 'space')
All inputs are finite; a program needn't handle non-finite values.
Results may differ from a plain program's by a relative error of at most 0.00017.
Values sent between devices are 32-bit elements; how exact they have to be, the bound alone decides.
A program may use at most 128 MiB of HBM per device.

v0:
```python
from functools import partial
import jax
import jax.numpy as jnp
from jax import lax
from jax.sharding import PartitionSpec as P

highest_mode = lax.Precision.HIGHEST


def shifted(shard, axis, by):
    devices = lax.axis_size(axis)
    pairs = [(i, i + by) for i in range(devices) if 0 <= i + by < devices]
    return lax.ppermute(shard, axis, pairs)


def apply_full(banded, current):
    count_tiles = banded.shape[0]
    tile_width = banded.shape[2]
    blocks = current.reshape(current.shape[0], count_tiles, tile_width, current.shape[2])
    empty_tile = jnp.zeros_like(blocks[:, :1])
    padded = jnp.concatenate([empty_tile, blocks, empty_tile], 1)
    stacked = jnp.concatenate([padded[:, :-2], padded[:, 1:-1], padded[:, 2:]], 2)
    result = jnp.einsum("crs,ncre->ncse", banded, stacked, precision=highest_mode)
    return result.reshape(current.shape)


def sweep(apply_step, inputs, entry, backward):
    length = inputs.shape[0]
    order = list(range(length - 1, -1, -1)) if backward else list(range(length))
    current = entry
    outputs = [entry] * length
    for moment in order:
        current = apply_step(current[None])[0] + inputs[moment]
        outputs[moment] = current
    return jnp.stack(outputs)


def carry_prefix(carry, tables, which, direction):
    total = carry
    for level in range(len(tables) + 1):
        reach = direction * (1 if level == 0 else 2 ** (level - 1))
        moved = shifted(total, "tm", reach)
        if level == 0:
            total = moved
        else:
            table = tables[level - 1][which]

            def term(start, count, table=table, moved=moved):
                return lax.dot_general(
                    table, moved, (((0,), (0,)), ((), ())), precision=highest_mode
                )

            total = total + lax.psum_scatter(
                term(jnp.int32(0), moved.shape[0] * lax.axis_size("space")),
                "space",
                scatter_dimension=0,
                tiled=True,
            )
    return total


def body(observed, gain, trans, dynamics, smooth_gain):
    steps, tile_width, members = observed.shape
    count_tiles = lax.axis_size("space")
    ranks = lax.axis_size("tm")
    place = lax.axis_index("tm")
    column = lax.axis_index("space")
    state_width = tile_width * count_tiles
    block_cols = state_width // ranks
    sections = (ranks - 1).bit_length()
    log_steps = steps.bit_length() - 1
    forcing = jnp.einsum("os,toe->tse", gain[0], observed, precision=highest_mode)
    full_trans, full_smooth, full_dynamics = (
        lax.all_gather(trans, "space", axis=0, tiled=True),
        lax.all_gather(smooth_gain, "space", axis=0, tiled=True),
        lax.all_gather(dynamics, "space", axis=0, tiled=True),
    )

    def first_block(full):
        target = place * block_cols // tile_width
        offset = place * block_cols % tile_width
        index = jnp.clip(target, 0, full.shape[0] - 1)
        slab = lax.dynamic_index_in_dim(full, index, 0, keepdims=False)
        row_start = jnp.clip(column - target + 1, 0, 2) * tile_width
        piece = lax.dynamic_slice(slab, (row_start, offset), (tile_width, block_cols))
        inside = (jnp.abs(column - target) <= 1).astype(jnp.float32)
        return piece * inside

    blocks = (first_block(full_trans), first_block(full_smooth))
    needed = []
    for level in range(log_steps + sections - 1):
        col_trans = lax.all_gather(blocks[0], "space", axis=0, tiled=True)
        col_smooth = lax.all_gather(blocks[1], "space", axis=0, tiled=True)
        blocks = (
            jnp.dot(
                lax.all_gather(blocks[0], "tm", axis=1, tiled=True),
                col_trans,
                precision=highest_mode,
            ),
            jnp.dot(
                lax.all_gather(blocks[1], "tm", axis=1, tiled=True),
                col_smooth,
                precision=highest_mode,
            ),
        )
        if level + 1 >= log_steps:
            needed.append(blocks)
    tables = []
    for pair in needed:
        tables.append(
            (
                lax.all_gather(pair[0], "tm", axis=1, tiled=True),
                lax.all_gather(pair[1], "tm", axis=1, tiled=True),
            )
        )
    final_moment = jnp.arange(steps)[:, None, None] == steps - 1
    at_end = jnp.logical_and(final_moment, place == ranks - 1)
    whole_forcing = lax.all_gather(forcing, "space", axis=1, tiled=True)
    zero_full = jnp.zeros((state_width, members), jnp.float32)
    step_trans = partial(apply_full, full_trans)
    step_smooth = partial(apply_full, full_smooth)
    trial = sweep(step_trans, whole_forcing, zero_full, False)
    own_tail = lax.dynamic_slice_in_dim(trial[steps - 1], column * tile_width, tile_width, 0)
    entry = carry_prefix(own_tail, tables, 0, 1)
    entry_full = lax.all_gather(entry, "space", axis=0, tiled=True)
    filtered_full = sweep(step_trans, whole_forcing, entry_full, False)
    mixed_full = apply_full(full_smooth, apply_full(full_dynamics, filtered_full))
    innovation_full = jnp.where(at_end, filtered_full, filtered_full - mixed_full)
    trial_back = sweep(step_smooth, innovation_full, zero_full, True)
    own_head = lax.dynamic_slice_in_dim(trial_back[0], column * tile_width, tile_width, 0)
    exit_state = carry_prefix(own_head, tables, 1, -1)
    exit_full = lax.all_gather(exit_state, "space", axis=0, tiled=True)
    smoothed_full = sweep(step_smooth, innovation_full, exit_full, True)
    filtered = lax.dynamic_slice_in_dim(filtered_full, column * tile_width, tile_width, 1)
    smoothed = lax.dynamic_slice_in_dim(smoothed_full, column * tile_width, tile_width, 1)
    return (filtered, smoothed)


def solution(mesh):
    return jax.shard_map(
        body,
        mesh=mesh,
        in_specs=(
            P("tm", "space", None),
            P("space", None, None),
            P("space", None, None),
            P("space", None, None),
            P("space", None, None),
        ),
        out_specs=(P("tm", "space", None), P("tm", "space", None)),
        check_vma=False,
    )
```

profile of v0, /device:TPU:0, one launch (start us, length us, event | category | flops | bytes accessed | tf_op | source)
XLA Modules:
  0.0 763.2 jit_solution(14386908536317861910)
XLA Ops:
  8.2 2.6 convolution_bitcast_fusion
  11.0 10.3 %all_gather.88 = f32[4,384,128]{2,1,0:T(8,128)S(1)} all-gather(f32[1,384,128]{2,1,0:T(8,128)} %param.7), channel_id=1, replica_groups=mesh['tm'=8,'space'=4] {'space'}, dimensions={0}, use_global_device_ids=true | all-gather | bytes 983040 | tf_op jit(solution)/shard_map/all_gather | solution.py:74
  21.4 7.7 %all-gather.1 = f32[1,512,64]{2,1,0:T(8,128)S(1)} all-gather(f32[1,128,64]{2,1,0:T(8,128)S(1)} %dynamic-slice_multiply_fusion.1), channel_id=3, replica_groups=mesh['tm'=8,'space'=4] {'space'}, dimensions={1}, use_global_device_ids=true | all-gather | bytes 163840 | tf_op jit(solution)/shard_map/all_gather | solution.py:92
  29.1 31.2 %all-gather = f32[1,128,512]{1,0,2:T(1,128)S(1)} all-gather(f32[1,128,64]{1,0,2:T(1,128)S(1)} %copy.199), channel_id=2, replica_groups=mesh['tm'=8,'space'=4] {'tm'}, dimensions={2}, use_global_device_ids=true | all-gather | bytes 294912 | tf_op jit(solution)/shard_map/all_gather | solution.py:96
  60.9 5.4 all_gather.93
  66.3 30.7 %all_gather.92 = f32[128,512]{0,1:T(8,128)S(1)} all-gather(f32[128,64]{0,1:T(8,128)S(1)} %fusion.174), channel_id=1, replica_groups=mesh['tm'=8,'space'=4] {'tm'}, dimensions={1}, use_global_device_ids=true | all-gather | bytes 294912 | tf_op jit(solution)/shard_map/all_gather | solution.py:96
  97.4 5.4 all_gather.95
  102.8 30.8 %all_gather.94 = f32[128,512]{0,1:T(8,128)S(1)} all-gather(f32[128,64]{0,1:T(8,128)S(1)} %fusion.211), channel_id=1, replica_groups=mesh['tm'=8,'space'=4] {'tm'}, dimensions={1}, use_global_device_ids=true | all-gather | bytes 294912 | tf_op jit(solution)/shard_map/all_gather | solution.py:96
  133.9 8.7 %all_gather.102 = f32[4,384,128]{2,1,0:T(8,128)S(1)} all-gather(f32[1,384,128]{2,1,0:T(8,128)S(1)} %copy-done.47), channel_id=1, replica_groups=mesh['tm'=8,'space'=4] {'space'}, dimensions={0}, use_global_device_ids=true | all-gather | bytes 983040 | tf_op jit(solution)/shard_map/all_gather | solution.py:75
  142.6 2.6 slice_bitcast_fusion.1
  147.7 2.6 fusion.19
  172.1 3.3 collective-permute-start
  175.4 30.7 %all_gather.96 = f32[128,512]{0,1:T(8,128)S(1)} all-gather(f32[128,64]{0,1:T(8,128)S(1)} %fusion.212), channel_id=1, replica_groups=mesh['tm'=8,'space'=4] {'tm'}, dimensions={1}, use_global_device_ids=true | all-gather | bytes 294912 | tf_op jit(solution)/shard_map/all_gather | solution.py:112
  206.1 5.4 all_gather.97
  216.3 5.8 all-gather.3
  222.1 31.7 %all_gather.98 = f32[128,512]{0,1:T(8,128)S(1)} all-gather(f32[128,64]{0,1:T(8,128)S(1)} %fusion.214), channel_id=1, replica_groups=mesh['tm'=8,'space'=4] {'tm'}, dimensions={1}, use_global_device_ids=true | all-gather | bytes 294912 | tf_op jit(solution)/shard_map/all_gather | solution.py:112
  253.8 30.7 %all-gather.2 = f32[1,128,512]{1,0,2:T(1,128)S(1)} all-gather(f32[1,128,64]{1,0,2:T(1,128)S(1)} %copy.255), channel_id=4, replica_groups=mesh['tm'=8,'space'=4] {'tm'}, dimensions={2}, use_global_device_ids=true | all-gather | bytes 294912 | tf_op jit(solution)/shard_map/all_gather | solution.py:101
  287.4 32.7 %all_gather.106 = f32[128,512]{0,1:T(8,128)} all-gather(f32[128,64]{0,1:T(8,128)S(1)} %fusion.172), channel_id=1, replica_groups=mesh['tm'=8,'space'=4] {'tm'}, dimensions={1}, use_global_device_ids=true | all-gather | bytes 294912 | tf_op jit(solution)/shard_map/all_gather | solution.py:101
  321.3 5.4 all_gather.99
  326.7 5.4 all_gather.107
  334.3 7.7 %reduce-scatter.9.cloned.1.call-done = f32[128,128]{0,1:T(8,128)} async-done(((f32[512,128]{0,1:T(8,128)}), f32[128,128]{0,1:T(8,128)}) %reduce-scatter.9.cloned.1.call-update) | async-done | bytes 65552 | tf_op jit(solution)/shard_map/reduce_scatter | solution.py:53
  343.4 4.3 collective-permute-start.3
  347.7 30.8 %all_gather.100 = f32[128,512]{0,1:T(8,128)S(1)} all-gather(f32[128,64]{0,1:T(8,128)S(1)} %fusion.216), channel_id=1, replica_groups=mesh['tm'=8,'space'=4] {'tm'}, dimensions={1}, use_global_device_ids=true | all-gather | bytes 294912 | tf_op jit(solution)/shard_map/all_gather | solution.py:112
  379.7 5.6 all_gather.109
  385.3 33.0 %all_gather.108 = f32[128,512]{0,1:T(8,128)} all-gather(f32[128,64]{0,1:T(8,128)} %fusion.218), channel_id=1, replica_groups=mesh['tm'=8,'space'=4] {'tm'}, dimensions={1}, use_global_device_ids=true | all-gather | bytes 294912 | tf_op jit(solution)/shard_map/all_gather | solution.py:101
  418.3 8.8 %all_gather.103 = f32[4,384,128]{2,1,0:T(8,128)} all-gather(f32[1,384,128]{2,1,0:T(8,128)} %param.8), channel_id=1, replica_groups=mesh['tm'=8,'space'=4] {'space'}, dimensions={0}, use_global_device_ids=true | all-gather | bytes 983040 | tf_op jit(solution)/shard_map/all_gather | solution.py:76
  428.0 6.3 all_gather.101
  449.8 3.1 bitcast_add_fusion.11
  487.4 4.3 fusion.15
  492.2 5.6 fusion.12
  501.9 2.9 subtract_select_fusion
  513.0 2.6 fusion.26
  517.5 2.6 fusion.27
  522.1 2.6 fusion.28
  526.7 2.6 fusion.29
  531.2 2.6 fusion.30
  535.8 2.6 fusion.31
  543.7 3.7 collective-permute-done.4
  548.7 30.8 %all_gather.110 = f32[128,512]{0,1:T(8,128)S(1)} all-gather(f32[128,64]{0,1:T(8,128)S(1)} %fusion.219), channel_id=1, replica_groups=mesh['tm'=8,'space'=4] {'tm'}, dimensions={1}, use_global_device_ids=true | all-gather | bytes 294912 | tf_op jit(solution)/shard_map/all_gather | solution.py:113
  580.6 5.4 all_gather.111
  586.3 13.7 %reduce-scatter.13.cloned.1.call-done = f32[128,128]{0,1:T(8,128)} async-done(((f32[512,128]{0,1:T(8,128)}), f32[128,128]{0,1:T(8,128)}) %reduce-scatter.13.cloned.1.call-update) | async-done | bytes 65552 | tf_op jit(solution)/shard_map/reduce_scatter | solution.py:53
  602.2 32.0 %all_gather.112 = f32[128,512]{0,1:T(8,128)S(1)} all-gather(f32[128,64]{0,1:T(8,128)S(1)} %fusion.221), channel_id=1, replica_groups=mesh['tm'=8,'space'=4] {'tm'}, dimensions={1}, use_global_device_ids=true | all-gather | bytes 294912 | tf_op jit(solution)/shard_map/all_gather | solution.py:113
  635.4 5.4 all_gather.113
  641.1 14.4 %reduce-scatter.15.cloned.1.call-done = f32[128,128]{0,1:T(8,128)} async-done(((f32[512,128]{0,1:T(8,128)}), f32[128,128]{0,1:T(8,128)}) %reduce-scatter.15.cloned.1.call-update) | async-done | bytes 65552 | tf_op jit(solution)/shard_map/reduce_scatter | solution.py:53
  657.6 32.0 %all_gather.114 = f32[128,512]{0,1:T(8,128)S(1)} all-gather(f32[128,64]{0,1:T(8,128)S(1)} %fusion.223), channel_id=1, replica_groups=mesh['tm'=8,'space'=4] {'tm'}, dimensions={1}, use_global_device_ids=true | all-gather | bytes 294912 | tf_op jit(solution)/shard_map/all_gather | solution.py:113
  694.7 16.3 %reduce-scatter.17.cloned.1.call-done = f32[128,128]{0,1:T(8,128)} async-done(((f32[512,128]{0,1:T(8,128)}), f32[128,128]{0,1:T(8,128)}) %reduce-scatter.17.cloned.1.call-update) | async-done | bytes 65552 | tf_op jit(solution)/shard_map/reduce_scatter | solution.py:53
  711.8 6.2 all_gather.115
  719.8 3.1 bitcast_add_fusion
  (291 shorter events, 167.7 us)
Async XLA Ops:
  7.2 135.4 %all-gather.6.cloned.1.call-start = ((), (), s32[]{:S(2)}) async-start(), calls=%async_computation.6 | async-start | bytes 2621440 | tf_op jit(solution)/shard_map/all_gather | solution.py:118
  10.9 274.3 %reduce-scatter.7.cloned.1.call-start = ((), (), s32[]{:S(2)}) async-start(), calls=%async_computation.7 | async-start | bytes 327680 | tf_op jit(solution)/shard_map/reduce_scatter | solution.py:53
  21.3 112.6 %copy-start.47 = (f32[1,384,128]{2,1,0:T(8,128)S(1)}, f32[1,384,128]{2,1,0:T(8,128)}, u32[]{:S(2)}) copy-start(f32[1,384,128]{2,1,0:T(8,128)} %param.9) | copy-start | bytes 589828
  133.6 11.7 %copy-start.3 = (f32[1,4,128,128]{3,2,1,0:T(8,128)}, f32[1,4,128,128]{3,2,1,0:T(8,128)S(1)}, u32[]{:S(2)}) copy-start(f32[1,4,128,128]{3,2,1,0:T(8,128)S(1)} %pad_slice_fusion.64) | copy-start | bytes 786436
  147.7 3.4 copy-start.9
  151.2 6.0 copy-start.8
  159.1 3.4 copy-start.31
  172.1 39.4 %collective-permute-start = (f32[128,128]{0,1:T(8,128)S(1)}, f32[128,128]{0,1:T(8,128)S(1)}, u32[]{:S(2)}, u32[]{:S(2)}) collective-permute-start(f32[128,128]{0,1:T(8,128)S(1)} %dynamic-slice_add_fusion.1), channel_id=1, source_target_pairs={{0,4},{4,8},{8,12},{12,16},{16,20},{20,24},{24,28},{1,5},{5,9},{9,... | collective-permute-start | bytes 196616 | tf_op jit(solution)/shard_map/ppermute | solution.py:13
  211.5 4.8 copy-start.48
  211.5 3.4 collective-permute-start.1
  216.1 125.9 %reduce-scatter.9.cloned.1.call-start = ((), (), s32[]{:S(2)}) async-start(), calls=%async_computation.8 | async-start | bytes 327680 | tf_op jit(solution)/shard_map/reduce_scatter | solution.py:53
  286.1 34.0 %collective-permute-start.2 = (f32[128,128]{0,1:T(8,128)S(1)}, f32[128,128]{0,1:T(8,128)S(1)}, u32[]{:S(2)}, u32[]{:S(2)}) collective-permute-start(f32[128,128]{0,1:T(8,128)S(1)} %add.374), channel_id=1, source_target_pairs={{0,8},{4,12},{8,16},{12,20},{16,24},{20,28},{1,9},{5,13},{9,17},{1... | collective-permute-start | bytes 196616 | tf_op jit(solution)/shard_map/ppermute | solution.py:13
  321.2 105.8 %reduce-scatter.11.cloned.1.call-start = ((), (), s32[]{:S(2)}) async-start(), calls=%async_computation.9 | async-start | bytes 327680 | tf_op jit(solution)/shard_map/reduce_scatter | solution.py:53
  343.4 35.1 %collective-permute-start.3 = (f32[128,128]{0,1:T(8,128)S(1)}, f32[128,128]{0,1:T(8,128)S(1)}, u32[]{:S(2)}, u32[]{:S(2)}) collective-permute-start(f32[128,128]{0,1:T(8,128)S(1)} %add.375), channel_id=1, source_target_pairs={{0,16},{4,20},{8,24},{12,28},{1,17},{5,21},{9,25},{13,29},{2,18},{... | collective-permute-start | bytes 196616 | tf_op jit(solution)/shard_map/ppermute | solution.py:13
  379.7 220.4 %reduce-scatter.13.cloned.1.call-start = ((), (), s32[]{:S(2)}) async-start(), calls=%async_computation.10 | async-start | bytes 327680 | tf_op jit(solution)/shard_map/reduce_scatter | solution.py:53
  476.2 3.5 copy-start.39
  476.2 4.2 copy-start.40
  476.2 4.9 copy-start.41
  477.6 4.2 copy-start.42
  477.7 4.9 copy-start.43
  477.8 5.5 copy-start.44
  484.7 2.7 copy-start.45
  504.8 3.2 copy-start.4
  513.0 3.5 copy-start.21
  517.5 3.5 copy-start.19
  522.1 3.5 copy-start.17
  526.6 3.5 copy-start.15
  531.2 4.6 copy-start.13
  535.8 4.3 copy-start.11
  541.1 6.2 collective-permute-start.4
  547.4 38.9 %copy-start.49 = (f32[128,128]{0,1:T(8,128)}, f32[128,128]{0,1:T(8,128)S(1)}, u32[]{:S(2)}) copy-start(f32[128,128]{0,1:T(8,128)S(1)} %collective-permute-done.4) | copy-start | bytes 196612
  547.4 32.1 %collective-permute-start.5 = (f32[128,128]{0,1:T(8,128)S(1)}, f32[128,128]{0,1:T(8,128)S(1)}, u32[]{:S(2)}, u32[]{:S(2)}) collective-permute-start(f32[128,128]{0,1:T(8,128)S(1)} %collective-permute-done.4), channel_id=1, source_target_pairs={{4,0},{8,4},{12,8},{16,12},{20,16},{24,20},{28,24},{5,1},{9,5},{13... | collective-permute-start | bytes 196616 | tf_op jit(solution)/shard_map/ppermute | solution.py:13
  580.5 74.9 %reduce-scatter.15.cloned.1.call-start = ((), (), s32[]{:S(2)}) async-start(), calls=%async_computation.11 | async-start | bytes 327680 | tf_op jit(solution)/shard_map/reduce_scatter | solution.py:53
  600.9 33.3 %collective-permute-start.6 = (f32[128,128]{0,1:T(8,128)S(1)}, f32[128,128]{0,1:T(8,128)S(1)}, u32[]{:S(2)}, u32[]{:S(2)}) collective-permute-start(f32[128,128]{0,1:T(8,128)S(1)} %add.400), channel_id=1, source_target_pairs={{8,0},{12,4},{16,8},{20,12},{24,16},{28,20},{9,1},{13,5},{17,9},{2... | collective-permute-start | bytes 196616 | tf_op jit(solution)/shard_map/ppermute | solution.py:13
  635.3 75.6 %reduce-scatter.17.cloned.1.call-start = ((), (), s32[]{:S(2)}) async-start(), calls=%async_computation.12 | async-start | bytes 327680 | tf_op jit(solution)/shard_map/reduce_scatter | solution.py:53
  656.3 33.3 %collective-permute-start.7 = (f32[128,128]{0,1:T(8,128)S(1)}, f32[128,128]{0,1:T(8,128)S(1)}, u32[]{:S(2)}, u32[]{:S(2)}) collective-permute-start(f32[128,128]{0,1:T(8,128)S(1)} %add.401), channel_id=1, source_target_pairs={{16,0},{20,4},{24,8},{28,12},{17,1},{21,5},{25,9},{29,13},{18,2},{... | collective-permute-start | bytes 196616 | tf_op jit(solution)/shard_map/ppermute | solution.py:13
  690.7 29.1 %copy-start.5 = (f32[1,512,128]{2,1,0:T(8,128)S(1)}, f32[1,512,128]{2,1,0:T(8,128)}, u32[]{:S(2)}) copy-start(f32[1,512,128]{2,1,0:T(8,128)} %copy.364) | copy-start | bytes 786436
  719.1 3.8 copy-start.22
  738.1 7.2 copy-start.32
  738.1 8.0 %copy-start.30 = (f32[4,128,128]{1,2,0:T(8,128)S(1)}, f32[4,128,128]{1,2,0:T(8,128)}, u32[]{:S(2)}) copy-start(f32[4,128,128]{1,2,0:T(8,128)} %get-tuple-element.125) | copy-start | bytes 786436
  738.1 8.9 %copy-start.29 = (f32[4,128,128]{1,2,0:T(8,128)S(1)}, f32[4,128,128]{1,2,0:T(8,128)}, u32[]{:S(2)}) copy-start(f32[4,128,128]{1,2,0:T(8,128)} %get-tuple-element.123) | copy-start | bytes 786436
  738.1 9.7 %copy-start.28 = (f32[4,128,128]{1,2,0:T(8,128)S(1)}, f32[4,128,128]{1,2,0:T(8,128)}, u32[]{:S(2)}) copy-start(f32[4,128,128]{1,2,0:T(8,128)} %get-tuple-element.121) | copy-start | bytes 786436
  740.0 8.7 %copy-start.27 = (f32[4,128,128]{1,2,0:T(8,128)S(1)}, f32[4,128,128]{1,2,0:T(8,128)}, u32[]{:S(2)}) copy-start(f32[4,128,128]{1,2,0:T(8,128)} %get-tuple-element.119) | copy-start | bytes 786436
  746.2 2.7 copy-start.33
  747.0 2.6 copy-start.34
  748.9 3.0 copy-start.37
  748.9 3.7 copy-start.38
  751.1 5.0 copy-start.1
  (17 other events, 26.4 us)
Sparse Core Ops, SparseCore 0:
  11.0 26.9 all-gather.5
  216.2 21.1 reduce-scatter.6
  321.4 20.5 reduce-scatter.8
  379.8 17.2 reduce-scatter.10
  580.7 19.3 reduce-scatter.12
  635.5 19.9 reduce-scatter.14
  690.8 20.0 reduce-scatter.16
where the time goes:
time: 769 us; the launch traced here: 763 us
  blocking collectives  474 us (62%)
  matrix products  95.9 us (12%)
  local copies, waits for them, and re-layouts  73.3 us (10%)
  waiting for transfers between devices  57.6 us (7%)
  other arithmetic  30.8 us (4%)
  starting transfers between devices  15.7 us (2%)
  between operations  15.5 us (2%)
    all_gather x3, blocking collectives, body(): lax.all_gather(blocks[1], 'tm', axis=1, tiled=True)  96.4 us
    all_gather x3, blocking collectives, body(): lax.all_gather(pair[1], 'tm', axis=1, tiled=True)  94.7 us
    all_gather x3, blocking collectives, body(): lax.all_gather(pair[0], 'tm', axis=1, tiled=True)  93.3 us
    all_gather x3, blocking collectives, body(): lax.all_gather(blocks[0], 'tm', axis=1, tiled=True)  92.7 us
    dot_general x34, matrix products, apply_full(): jnp.einsum('crs,ncre->ncse', banded, stacked, precision=highest_mode)  80.7 us
    reduce_scatter x6, waiting for transfers between devices, carry_prefix(): lax.psum_scatter(term(jnp.int32(0), moved.shape[0] * lax.axis_size('space...  52.1 us
    all_gather x5, blocking collectives, body(): col_trans = lax.all_gather(blocks[0], 'space', axis=0, tiled=True)  29.3 us
    all_gather x5, blocking collectives, body(): col_smooth = lax.all_gather(blocks[1], 'space', axis=0, tiled=True)  27.6 us
  transfers between devices with their start and end apart: 15, of which 6 were waited for; matrix products, arithmetic and copies ran while one was open for 1% of the time, Pallas kernels for 0%

commit v1 on v0

--- a/solution.py
+++ b/solution.py
@@ -109,7 +109,7 @@
     for pair in needed:
         tables.append(
             (
-                lax.all_gather(pair[0], "tm", axis=1, tiled=True),
+                jnp.concatenate(lax.all_gather(pair[0], "tm"), axis=1),
                 lax.all_gather(pair[1], "tm", axis=1, tiled=True),
             )
         )

time: 769 us -> 847 us (1.10)
  blocking collectives: 474 us -> 546 us
    all_gather x3 -> x5, blocking collectives: 92.7 us -> 154 us  [body(): lax.all_gather(blocks[0], 'tm', axis=1, tiled=True)]
  transfers between devices with their start and end apart: 15 -> 15, of which waited for: 6 -> 5; matrix products, arithmetic and copies ran while one was open for 1% -> 2% of each run, Pallas kernels for 0% -> 0%
where the time goes in v1:
time: 847 us; the launch traced here: 841 us
  blocking collectives  546 us (64%)
  matrix products  98.7 us (12%)
  local copies, waits for them, and re-layouts  76.2 us (9%)
  waiting for transfers between devices  57.8 us (7%)
  other arithmetic  31 us (4%)
  between operations  15.5 us (2%)
  starting transfers between devices  15 us (2%)
    all_gather x5, blocking collectives, body(): lax.all_gather(blocks[0], 'tm', axis=1, tiled=True)  154 us
    all_gather x3, blocking collectives, body(): lax.all_gather(blocks[1], 'tm', axis=1, tiled=True)  100 us
    all_gather x3, blocking collectives, body(): lax.all_gather(pair[1], 'tm', axis=1, tiled=True)  96.4 us
    all_gather x3, blocking collectives, body(): lax.all_gather(pair[0], 'tm')  94.7 us
    dot_general x34, matrix products, apply_full(): jnp.einsum('crs,ncre->ncse', banded, stacked, precision=highest_mode)  80.1 us
    reduce_scatter x6, waiting for transfers between devices, carry_prefix(): lax.psum_scatter(term(jnp.int32(0), moved.shape[0] * lax.axis_size('space...  53.6 us
    all_gather x5, blocking collectives, body(): col_trans = lax.all_gather(blocks[0], 'space', axis=0, tiled=True)  28.2 us
    all_gather x5, blocking collectives, body(): col_smooth = lax.all_gather(blocks[1], 'space', axis=0, tiled=True)  27.9 us
  transfers between devices with their start and end apart: 15, of which 5 were waited for; matrix products, arithmetic and copies ran while one was open for 2% of the time, Pallas kernels for 0%

profile of v1, /device:TPU:0, one launch (start us, length us, event | category | flops | bytes accessed | tf_op | source)
XLA Modules:
  0.0 840.6 jit_solution(38884040996748237)
XLA Ops:
  8.2 2.6 convolution_bitcast_fusion
  11.0 10.3 %all_gather.101 = f32[4,384,128]{2,1,0:T(8,128)S(1)} all-gather(f32[1,384,128]{2,1,0:T(8,128)} %param.7), channel_id=1, replica_groups=mesh['tm'=8,'space'=4] {'space'}, dimensions={0}, use_global_device_ids=true | all-gather | bytes 983040 | tf_op jit(solution)/shard_map/all_gather | solution.py:74
  21.4 13.3 %all_gather.120 = f32[4,384,128]{2,1,0:T(8,128)S(1)} all-gather(f32[1,384,128]{2,1,0:T(8,128)S(1)} %copy-done.45), channel_id=1, replica_groups=mesh['tm'=8,'space'=4] {'space'}, dimensions={0}, use_global_device_ids=true | all-gather | bytes 983040 | tf_op jit(solution)/shard_map/all_gather | solution.py:75
  34.9 6.3 all-gather.1
  41.2 30.9 %all-gather = f32[1,128,512]{1,0,2:T(1,128)S(1)} all-gather(f32[1,128,64]{1,0,2:T(1,128)S(1)} %copy.277), channel_id=2, replica_groups=mesh['tm'=8,'space'=4] {'tm'}, dimensions={2}, use_global_device_ids=true | all-gather | bytes 294912 | tf_op jit(solution)/shard_map/all_gather | solution.py:96
  72.7 5.4 all_gather.106
  78.1 30.7 %all_gather.105 = f32[128,512]{0,1:T(8,128)S(1)} all-gather(f32[128,64]{0,1:T(8,128)S(1)} %fusion.174), channel_id=1, replica_groups=mesh['tm'=8,'space'=4] {'tm'}, dimensions={1}, use_global_device_ids=true | all-gather | bytes 294912 | tf_op jit(solution)/shard_map/all_gather | solution.py:96
  109.1 5.4 all_gather.108
  114.6 30.8 %all_gather.107 = f32[128,512]{0,1:T(8,128)S(1)} all-gather(f32[128,64]{0,1:T(8,128)S(1)} %fusion.211), channel_id=1, replica_groups=mesh['tm'=8,'space'=4] {'tm'}, dimensions={1}, use_global_device_ids=true | all-gather | bytes 294912 | tf_op jit(solution)/shard_map/all_gather | solution.py:96
  145.6 5.4 all_gather.112
  151.0 30.7 %all_gather.111 = f32[128,512]{0,1:T(8,128)S(1)} all-gather(f32[128,64]{0,1:T(8,128)S(1)} %fusion.212), channel_id=1, replica_groups=mesh['tm'=8,'space'=4] {'tm'}, dimensions={1}, use_global_device_ids=true | all-gather | bytes 294912 | tf_op jit(solution)/shard_map/all_gather | solution.py:96
  181.8 31.2 %all-gather.2 = f32[1024,64]{0,1:T(8,128)S(1)} all-gather(f32[128,64]{0,1:T(8,128)S(1)} %fusion.212), channel_id=4, replica_groups=mesh['tm'=8,'space'=4] {'tm'}, dimensions={0}, use_global_device_ids=true | all-gather | bytes 294912 | tf_op jit(solution)/shard_map/all_gather | solution.py:112
  214.0 2.6 slice_bitcast_fusion.1
  227.2 2.6 fusion.21
  244.6 3.4 collective-permute-start
  248.0 32.8 %all-gather.3 = f32[1024,64]{0,1:T(8,128)} all-gather(f32[128,64]{0,1:T(8,128)S(1)} %fusion.214), channel_id=5, replica_groups=mesh['tm'=8,'space'=4] {'tm'}, dimensions={0}, use_global_device_ids=true | all-gather | bytes 294912 | tf_op jit(solution)/shard_map/all_gather | solution.py:112
  282.3 32.7 %all-gather.5 = f32[1,128,512]{1,0,2:T(1,128)} all-gather(f32[1,128,64]{1,0,2:T(1,128)S(1)} %copy.336), channel_id=7, replica_groups=mesh['tm'=8,'space'=4] {'tm'}, dimensions={2}, use_global_device_ids=true | all-gather | bytes 294912 | tf_op jit(solution)/shard_map/all_gather | solution.py:101
  317.2 5.8 all-gather.6
  326.8 8.8 %reduce-scatter.7.cloned.1.call-done = f32[128,128]{0,1:T(8,128)} async-done(((f32[512,128]{0,1:T(8,128)}), f32[128,128]{0,1:T(8,128)}) %reduce-scatter.7.cloned.1.call-update) | async-done | bytes 65552 | tf_op jit(solution)/shard_map/reduce_scatter | solution.py:53
  336.5 3.4 collective-permute-start.2
  339.9 30.7 %all_gather.115 = f32[128,512]{0,1:T(8,128)S(1)} all-gather(f32[128,64]{0,1:T(8,128)S(1)} %fusion.214), channel_id=1, replica_groups=mesh['tm'=8,'space'=4] {'tm'}, dimensions={1}, use_global_device_ids=true | all-gather | bytes 294912 | tf_op jit(solution)/shard_map/all_gather | solution.py:96
  370.7 5.6 all_gather.116
  378.7 5.6 all_gather.125
  384.3 33.0 %all_gather.124 = f32[128,512]{0,1:T(8,128)} all-gather(f32[128,64]{0,1:T(8,128)} %fusion.172), channel_id=1, replica_groups=mesh['tm'=8,'space'=4] {'tm'}, dimensions={1}, use_global_device_ids=true | all-gather | bytes 294912 | tf_op jit(solution)/shard_map/all_gather | solution.py:101
  417.3 30.8 %all-gather.4 = f32[1024,64]{0,1:T(8,128)S(1)} all-gather(f32[128,64]{0,1:T(8,128)S(1)} %fusion.216), channel_id=6, replica_groups=mesh['tm'=8,'space'=4] {'tm'}, dimensions={0}, use_global_device_ids=true | all-gather | bytes 294912 | tf_op jit(solution)/shard_map/all_gather | solution.py:112
  453.4 5.6 all_gather.127
  459.0 34.6 %all_gather.126 = f32[128,512]{0,1:T(8,128)} all-gather(f32[128,64]{0,1:T(8,128)} %fusion.218), channel_id=1, replica_groups=mesh['tm'=8,'space'=4] {'tm'}, dimensions={1}, use_global_device_ids=true | all-gather | bytes 294912 | tf_op jit(solution)/shard_map/all_gather | solution.py:101
  493.6 8.7 %all_gather.121 = f32[4,384,128]{2,1,0:T(8,128)} all-gather(f32[1,384,128]{2,1,0:T(8,128)} %param.8), channel_id=1, replica_groups=mesh['tm'=8,'space'=4] {'space'}, dimensions={0}, use_global_device_ids=true | all-gather | bytes 983040 | tf_op jit(solution)/shard_map/all_gather | solution.py:76
  503.2 6.3 all_gather.119
  525.1 3.1 bitcast_add_fusion.11
  532.9 3.1 bitcast_add_fusion.10
  566.5 4.3 fusion.15
  571.3 5.6 fusion.12
  580.9 2.9 subtract_select_fusion
  592.0 2.6 fusion.26
  601.1 2.6 fusion.28
  605.7 2.6 fusion.29
  610.3 2.6 fusion.30
  622.6 4.1 collective-permute-done.4
  627.9 32.5 %all_gather.128 = f32[128,512]{0,1:T(8,128)S(1)} all-gather(f32[128,64]{0,1:T(8,128)S(1)} %fusion.219), channel_id=1, replica_groups=mesh['tm'=8,'space'=4] {'tm'}, dimensions={1}, use_global_device_ids=true | all-gather | bytes 294912 | tf_op jit(solution)/shard_map/all_gather | solution.py:113
  661.6 5.4 all_gather.129
  667.3 14.1 %reduce-scatter.13.cloned.1.call-done = f32[128,128]{0,1:T(8,128)} async-done(((f32[512,128]{0,1:T(8,128)}), f32[128,128]{0,1:T(8,128)}) %reduce-scatter.13.cloned.1.call-update) | async-done | bytes 65552 | tf_op jit(solution)/shard_map/reduce_scatter | solution.py:53
  683.6 32.0 %all_gather.130 = f32[128,512]{0,1:T(8,128)S(1)} all-gather(f32[128,64]{0,1:T(8,128)S(1)} %fusion.221), channel_id=1, replica_groups=mesh['tm'=8,'space'=4] {'tm'}, dimensions={1}, use_global_device_ids=true | all-gather | bytes 294912 | tf_op jit(solution)/shard_map/all_gather | solution.py:113
  716.7 5.4 all_gather.131
  722.4 14.4 %reduce-scatter.15.cloned.1.call-done = f32[128,128]{0,1:T(8,128)} async-done(((f32[512,128]{0,1:T(8,128)}), f32[128,128]{0,1:T(8,128)}) %reduce-scatter.15.cloned.1.call-update) | async-done | bytes 65552 | tf_op jit(solution)/shard_map/reduce_scatter | solution.py:53
  739.0 31.9 %all_gather.132 = f32[128,512]{0,1:T(8,128)S(1)} all-gather(f32[128,64]{0,1:T(8,128)S(1)} %fusion.223), channel_id=1, replica_groups=mesh['tm'=8,'space'=4] {'tm'}, dimensions={1}, use_global_device_ids=true | all-gather | bytes 294912 | tf_op jit(solution)/shard_map/all_gather | solution.py:113
  776.0 16.3 %reduce-scatter.17.cloned.1.call-done = f32[128,128]{0,1:T(8,128)} async-done(((f32[512,128]{0,1:T(8,128)}), f32[128,128]{0,1:T(8,128)}) %reduce-scatter.17.cloned.1.call-update) | async-done | bytes 65552 | tf_op jit(solution)/shard_map/reduce_scatter | solution.py:53
  793.1 6.2 all_gather.133
  (292 shorter events, 177.2 us)
Async XLA Ops:
  7.2 14.2 %copy-start.45 = (f32[1,384,128]{2,1,0:T(8,128)S(1)}, f32[1,384,128]{2,1,0:T(8,128)}, u32[]{:S(2)}) copy-start(f32[1,384,128]{2,1,0:T(8,128)} %param.9) | copy-start | bytes 589828
  7.2 206.8 %all-gather.9.cloned.1.call-start = ((), (), s32[]{:S(2)}) async-start(), calls=%async_computation.6 | async-start | bytes 2621440 | tf_op jit(solution)/shard_map/all_gather | solution.py:118
  10.9 324.8 %reduce-scatter.7.cloned.1.call-start = ((), (), s32[]{:S(2)}) async-start(), calls=%async_computation.7 | async-start | bytes 327680 | tf_op jit(solution)/shard_map/reduce_scatter | solution.py:53
  213.3 126.6 %copy-start.42 = (f32[128,64]{0,1:T(8,128)}, f32[128,64]{0,1:T(8,128)S(1)}, u32[]{:S(2)}) copy-start(f32[128,64]{0,1:T(8,128)S(1)} %fusion.214) | copy-start | bytes 98308
  219.2 6.1 copy-start.7
  222.7 3.4 copy-start.6
  227.2 6.0 copy-start.5
  227.2 3.4 copy-start.28
  244.6 36.2 %collective-permute-start = (f32[128,128]{0,1:T(8,128)S(1)}, f32[128,128]{0,1:T(8,128)S(1)}, u32[]{:S(2)}, u32[]{:S(2)}) collective-permute-start(f32[128,128]{0,1:T(8,128)S(1)} %dynamic-slice_add_fusion.1), channel_id=1, source_target_pairs={{0,4},{4,8},{8,12},{12,16},{16,20},{20,24},{24,28},{1,5},{5,9},{9,... | collective-permute-start | bytes 196616 | tf_op jit(solution)/shard_map/ppermute | solution.py:13
  280.8 36.3 %copy-start.46 = (f32[128,128]{0,1:T(8,128)}, f32[128,128]{0,1:T(8,128)S(1)}, u32[]{:S(2)}) copy-start(f32[128,128]{0,1:T(8,128)S(1)} %collective-permute-done) | copy-start | bytes 196612
  280.8 34.3 %collective-permute-start.1 = (f32[128,128]{0,1:T(8,128)S(1)}, f32[128,128]{0,1:T(8,128)S(1)}, u32[]{:S(2)}, u32[]{:S(2)}) collective-permute-start(f32[128,128]{0,1:T(8,128)S(1)} %collective-permute-done), channel_id=1, source_target_pairs={{0,4},{4,8},{8,12},{12,16},{16,20},{20,24},{24,28},{1,5},{5,9},{9,... | collective-permute-start | bytes 196616 | tf_op jit(solution)/shard_map/ppermute | solution.py:13
  317.1 131.0 %reduce-scatter.9.cloned.1.call-start = ((), (), s32[]{:S(2)}) async-start(), calls=%async_computation.8 | async-start | bytes 327680 | tf_op jit(solution)/shard_map/reduce_scatter | solution.py:53
  336.5 34.2 %copy-start.43 = (f32[128,128]{0,1:T(8,128)}, f32[128,128]{0,1:T(8,128)S(1)}, u32[]{:S(2)}) copy-start(f32[128,128]{0,1:T(8,128)S(1)} %add.374) | copy-start | bytes 196612
  336.5 39.8 %collective-permute-start.2 = (f32[128,128]{0,1:T(8,128)S(1)}, f32[128,128]{0,1:T(8,128)S(1)}, u32[]{:S(2)}, u32[]{:S(2)}) collective-permute-start(f32[128,128]{0,1:T(8,128)S(1)} %add.374), channel_id=1, source_target_pairs={{0,8},{4,12},{8,16},{12,20},{16,24},{20,28},{1,9},{5,13},{9,17},{1... | collective-permute-start | bytes 196616 | tf_op jit(solution)/shard_map/ppermute | solution.py:13
  378.4 124.0 %reduce-scatter.11.cloned.1.call-start = ((), (), s32[]{:S(2)}) async-start(), calls=%async_computation.9 | async-start | bytes 327680 | tf_op jit(solution)/shard_map/reduce_scatter | solution.py:53
  449.0 3.2 copy-start.44
  449.1 3.2 collective-permute-start.3
  453.3 228.1 %reduce-scatter.13.cloned.1.call-start = ((), (), s32[]{:S(2)}) async-start(), calls=%async_computation.10 | async-start | bytes 327680 | tf_op jit(solution)/shard_map/reduce_scatter | solution.py:53
  555.2 3.5 copy-start.35
  555.2 4.3 copy-start.36
  556.6 3.5 copy-start.37
  556.6 4.3 copy-start.38
  556.6 5.0 copy-start.39
  556.8 5.6 copy-start.40
  563.8 2.7 copy-start.41
  592.0 3.5 copy-start.19
  596.6 3.5 copy-start.17
  601.1 3.5 copy-start.15
  605.7 3.5 copy-start.13
  610.2 3.5 copy-start.11
  614.8 4.3 copy-start.9
  620.0 6.6 collective-permute-start.4
  626.7 40.7 %copy-start.47 = (f32[128,128]{0,1:T(8,128)}, f32[128,128]{0,1:T(8,128)S(1)}, u32[]{:S(2)}) copy-start(f32[128,128]{0,1:T(8,128)S(1)} %collective-permute-done.4) | copy-start | bytes 196612
  626.7 33.8 %collective-permute-start.5 = (f32[128,128]{0,1:T(8,128)S(1)}, f32[128,128]{0,1:T(8,128)S(1)}, u32[]{:S(2)}, u32[]{:S(2)}) collective-permute-start(f32[128,128]{0,1:T(8,128)S(1)} %collective-permute-done.4), channel_id=1, source_target_pairs={{4,0},{8,4},{12,8},{16,12},{20,16},{24,20},{28,24},{5,1},{9,5},{13... | collective-permute-start | bytes 196616 | tf_op jit(solution)/shard_map/ppermute | solution.py:13
  661.5 75.3 %reduce-scatter.15.cloned.1.call-start = ((), (), s32[]{:S(2)}) async-start(), calls=%async_computation.11 | async-start | bytes 327680 | tf_op jit(solution)/shard_map/reduce_scatter | solution.py:53
  682.3 33.3 %collective-permute-start.6 = (f32[128,128]{0,1:T(8,128)S(1)}, f32[128,128]{0,1:T(8,128)S(1)}, u32[]{:S(2)}, u32[]{:S(2)}) collective-permute-start(f32[128,128]{0,1:T(8,128)S(1)} %add.400), channel_id=1, source_target_pairs={{8,0},{12,4},{16,8},{20,12},{24,16},{28,20},{9,1},{13,5},{17,9},{2... | collective-permute-start | bytes 196616 | tf_op jit(solution)/shard_map/ppermute | solution.py:13
  716.7 75.6 %reduce-scatter.17.cloned.1.call-start = ((), (), s32[]{:S(2)}) async-start(), calls=%async_computation.12 | async-start | bytes 327680 | tf_op jit(solution)/shard_map/reduce_scatter | solution.py:53
  737.7 33.2 %collective-permute-start.7 = (f32[128,128]{0,1:T(8,128)S(1)}, f32[128,128]{0,1:T(8,128)S(1)}, u32[]{:S(2)}, u32[]{:S(2)}) collective-permute-start(f32[128,128]{0,1:T(8,128)S(1)} %add.401), channel_id=1, source_target_pairs={{16,0},{20,4},{24,8},{28,12},{17,1},{21,5},{25,9},{29,13},{18,2},{... | collective-permute-start | bytes 196616 | tf_op jit(solution)/shard_map/ppermute | solution.py:13
  772.0 28.5 %copy-start.3 = (f32[1,512,128]{2,1,0:T(8,128)S(1)}, f32[1,512,128]{2,1,0:T(8,128)}, u32[]{:S(2)}) copy-start(f32[1,512,128]{2,1,0:T(8,128)} %copy.445) | copy-start | bytes 786436
  816.5 6.2 copy-start.27
  816.5 7.0 copy-start.26
  816.5 7.8 copy-start.25
  817.4 8.7 %copy-start.24 = (f32[4,128,128]{1,2,0:T(8,128)S(1)}, f32[4,128,128]{1,2,0:T(8,128)}, u32[]{:S(2)}) copy-start(f32[4,128,128]{1,2,0:T(8,128)} %get-tuple-element.121) | copy-start | bytes 786436
  823.5 2.7 copy-start.29
  824.4 2.6 copy-start.30
  826.2 3.0 copy-start.33
  826.2 3.7 copy-start.34
  828.5 5.1 copy-start.1
  (15 other events, 26.6 us)
Sparse Core Ops, SparseCore 0:
  11.0 30.1 all-gather.8
  317.3 18.3 reduce-scatter.6
  378.5 18.1 reduce-scatter.8
  453.5 22.1 reduce-scatter.10
  661.7 19.6 reduce-scatter.12
  716.8 19.9 reduce-scatter.14
  772.2 20.0 reduce-scatter.16
